TPU v7x, 32 devices: a whole 2x2x4 slice. The times are simulated.
32 devices in a mesh: freq: 4 (over y, core), lat: 8 (over z, x).
Axes of the slice: x: 2, y: 2, z: 4, core: 2. Of those that a mesh axis runs over, the one named last changes fastest.
Arguments:
- spectra: float32 [2, 4, 32768], P(None, None, ('freq', 'lat')), may hold values from -6 to 6
- tile_route: int32 [32768, 1], P(('freq', 'lat')), may hold values from 0 to 255; in each aligned block of 1024 rows (0 to 1023, 1024 to 2047, ...) at most 8 rows name the same one
- bin_in_tile: int32 [32768], P(('freq', 'lat')), may hold values from 0 to 1023
- trace_offset: float32 [2, 32768], P(None, ('freq', 'lat')), may hold values from -0.5 to 0.5
- weights: float32 [32768], P(('freq', 'lat')), may hold values from 0.2 to 5
- frequency: float32 [4], P('freq'), may hold values from 0.5 to 1.5
- slowness: float32 [2, 8], replicated, may hold values from 0.6 to 1.6
- vel_index: int32 [2, 512, 512], P(None, 'lat'), may hold values from 0 to 7
Outputs:
- wavefield: float32 [2, 4, 512, 512], P(None, 'freq', 'lat')
- depth_image: float32 [2, 512, 512], P(None, 'lat', 'freq')
Inputs may be any that keep to these rules, and one draw needn't show every extreme that they name: `tile_route`: tiles of 32 x 32 bins, numbered row by row over the grid; among the rows of one device no tile is named by more than 8 traces. `bin_in_tile`: row * 32 + column of the bin within the tile.
All inputs are finite; a program needn't handle non-finite values.
Results may differ from a plain program's by a relative error of at most 0.0003.
Values sent between devices are 32-bit elements; how exact they have to be, the bound alone decides.
A program may use at most 64 MiB of HBM per device.

v0:
```python
import math
import jax
import jax.numpy as jnp
from jax import lax
from jax.sharding import PartitionSpec as P

NX = 512
NY = 512
TB = 32
MODES = 8
NSTEPS = 2
NREF = 2
NVEL = 8
TILES = 256
CAP = 8
damping = 1.0
depth_step = 1.0
block_tiles = 8


def dft_real(length, direction):
    counter = jnp.arange(length)
    angles = (
        2.0 * math.pi / length * (counter[:, None] * counter[None, :] % length).astype(jnp.float32)
    )
    cosine = jnp.cos(angles)
    sine_part = direction * jnp.sin(angles)
    return jnp.stack([jnp.stack([cosine, sine_part], 1), jnp.stack([-sine_part, cosine], 1)], 0)


def twiddle(full_length, first_len, second_len, direction):
    first_at = jnp.arange(first_len)[:, None]
    second_at = jnp.arange(second_len)[None, :]
    angles = 2.0 * math.pi / full_length * (first_at * second_at % full_length).astype(jnp.float32)
    return (jnp.cos(angles), direction * jnp.sin(angles))


def complex_scale(values, cosine, sine_part, part_axis):
    real_part = jnp.take(values, 0, axis=part_axis)
    imag_part = jnp.take(values, 1, axis=part_axis)
    return jnp.stack(
        [real_part * cosine - imag_part * sine_part, real_part * sine_part + imag_part * cosine],
        part_axis,
    )


def normal_terms(trace_meta, values_in):
    slot_count = trace_meta.shape[-1]
    tile_count = slot_count // CAP
    block_width = block_tiles * CAP
    mode_ids = jnp.arange(MODES).astype(jnp.float32)[:, None, None, None, None]

    def one_block(block_at):
        meta_part = lax.dynamic_slice_in_dim(trace_meta, block_at * block_width, block_width, 4)
        data_part = lax.dynamic_slice_in_dim(values_in, block_at * block_width, block_width, 4)
        meta_part = meta_part.reshape(meta_part.shape[:4] + (block_tiles, CAP))
        data_part = data_part.reshape(data_part.shape[:4] + (block_tiles, CAP))
        weight_part = meta_part[0, :, 0]
        along_x = jnp.cos(math.pi * mode_ids * (meta_part[1, :, 0][None] + 0.5) / TB)
        along_y = jnp.cos(math.pi * mode_ids * (meta_part[2, :, 0][None] + 0.5) / TB)
        basis_vals = (along_x[:, None] * along_y[None, :]).reshape(
            (MODES * MODES,) + weight_part.shape
        )
        weighted = basis_vals * weight_part[None]
        normal = jnp.einsum(
            "iabgc,jabgc->gij", weighted, basis_vals, precision=lax.Precision.HIGHEST
        )
        right_side = jnp.einsum(
            "iabgc,paqbgc->gipq", weighted, data_part, precision=lax.Precision.HIGHEST
        )
        return (normal, right_side)

    normal, right_side = lax.map(one_block, jnp.arange(tile_count // block_tiles))
    normal = normal.reshape(tile_count, MODES * MODES, MODES * MODES)
    right_side = right_side.reshape((tile_count, MODES * MODES) + right_side.shape[3:])
    return (normal, right_side)


def fit_grid(normal, right_side, row_count):
    tile_count = normal.shape[0]
    system = normal + damping * jnp.eye(MODES * MODES, dtype=jnp.float32)
    factor = jnp.linalg.cholesky(system)
    flat_rhs = right_side.reshape(tile_count, MODES * MODES, -1)
    middle = jax.scipy.linalg.solve_triangular(factor, flat_rhs, lower=True)
    coeffs = jax.scipy.linalg.solve_triangular(factor, middle, lower=True, trans="T")
    coeffs = coeffs.reshape(row_count // TB, NY // TB, MODES, MODES, 2, -1)
    cell_pos = jnp.arange(TB).astype(jnp.float32)
    cos_table = jnp.cos(
        math.pi * jnp.arange(MODES).astype(jnp.float32)[:, None] * (cell_pos[None, :] + 0.5) / TB
    )
    viewed = jnp.einsum(
        "xyabpq,ai,bj->pqxiyj", coeffs, cos_table, cos_table, precision=lax.Precision.HIGHEST
    )
    return viewed.reshape(2, viewed.shape[1], row_count, NY)


def local(spectra, tile_route, bin_in_tile, trace_offset, weights, frequency, slowness, vel_index):
    lat_count = lax.axis_size("lat")
    row_count = vel_index.shape[1]
    tile_dev = TILES // lat_count
    slot_count = tile_dev * CAP
    total_freqs = spectra.shape[1]
    tile_id = tile_route[:, 0]
    trace_count = tile_id.shape[0]
    ranking = jnp.argsort(tile_id, stable=True)
    sorted_tiles = tile_id[ranking]
    firsts = jnp.searchsorted(sorted_tiles, sorted_tiles, side="left")
    position = sorted_tiles * CAP + jnp.arange(trace_count, dtype=jnp.int32) - firsts
    slot_of = jnp.zeros((trace_count,), jnp.int32).at[ranking].set(position)
    owner_lat = slot_of // slot_count
    within = slot_of % slot_count
    cell_x = (bin_in_tile // TB).astype(jnp.float32) + trace_offset[0]
    cell_y = (bin_in_tile % TB).astype(jnp.float32) + trace_offset[1]
    trace_meta = jnp.stack([weights, cell_x, cell_y], 0)
    meta_buf = (
        jnp.zeros((3, lat_count, slot_count), jnp.float32).at[:, owner_lat, within].set(trace_meta)
    )
    spec_buf = (
        jnp.zeros((2, total_freqs, lat_count, slot_count), jnp.float32)
        .at[:, :, owner_lat, within]
        .set(spectra)
    )
    got_spec, got_meta = (
        lax.all_to_all(spec_buf, "lat", split_axis=2, concat_axis=2, tiled=True),
        lax.all_to_all(meta_buf[:, None], "lat", split_axis=2, concat_axis=2, tiled=True),
    )
    normal, right_side = normal_terms(got_meta[:, None], got_spec[:, None])
    normal = lax.psum(normal, "freq")
    right_side = lax.psum_scatter(right_side, "freq", scatter_dimension=3, tiled=True)
    wave_field = fit_grid(normal, right_side, row_count)
    len_x = NX // 8
    len_y = NY // 8
    w8_fwd = dft_real(8, -1.0)
    w8_inv = dft_real(8, 1.0)
    wx_fwd = dft_real(len_x, -1.0)
    wx_inv = dft_real(len_x, 1.0)
    wy_fwd = dft_real(len_y, -1.0)
    wy_inv = dft_real(len_y, 1.0)
    twx_fwd = twiddle(NX, 8, len_x, -1.0)
    twx_inv = twiddle(NX, 8, len_x, 1.0)
    twy_fwd = twiddle(NY, 8, len_y, -1.0)
    twy_inv = twiddle(NY, 8, len_y, 1.0)
    inverse_scale = 1.0 / (NX * NY)

    def forward_x(columns):
        dims_of = columns.shape
        viewed = columns.reshape(dims_of[:4] + (8, len_x))
        section_a = jnp.einsum(
            "phkqmn,pmsl->shkqln", viewed, w8_fwd, precision=lax.Precision.HIGHEST
        )
        section_b = complex_scale(section_a, twx_fwd[0], twx_fwd[1], 0)
        return jnp.einsum("shkqln,snto->thkqlo", section_b, wx_fwd, precision=lax.Precision.HIGHEST)

    def inverse_y(columns):
        section_c = jnp.einsum(
            "jthkqr,thsn->jsqrkn", columns, wy_inv, precision=lax.Precision.HIGHEST
        )
        section_b = complex_scale(section_c, twy_inv[0], twy_inv[1], 1)
        section_a = jnp.einsum(
            "jsqrkn,skpm->jpqrmn", section_b, w8_inv, precision=lax.Precision.HIGHEST
        )
        return section_a.reshape(section_a.shape[:4] + (NY,)) * inverse_scale

    lat_at = lax.axis_index("lat")
    ky_band = len_y // lat_count
    ky_index = jnp.arange(8)[None, :] + 8 * (lat_at * ky_band + jnp.arange(ky_band)[:, None])
    ky_signed = jnp.where(ky_index >= NY // 2, ky_index - NY, ky_index)
    ky_vals = 2.0 * math.pi / NY * ky_signed.astype(jnp.float32)
    kx_index = jnp.arange(8)[:, None] + 8 * jnp.arange(len_x)[None, :]
    kx_signed = jnp.where(kx_index >= NX // 2, kx_index - NX, kx_index)
    kx_vals = 2.0 * math.pi / NX * kx_signed.astype(jnp.float32)
    ky_sq = (ky_vals * ky_vals)[None, :, :, None, None, None]
    kx_sq = (kx_vals * kx_vals)[None, None, None, None, :, :]
    per_group = NVEL // NREF
    image_rows = []
    for depth_at in range(NSTEPS):
        table_row = slowness[depth_at]
        references = table_row.reshape(NREF, per_group).mean(axis=1)
        forward_dims_of = wave_field.shape
        forward_viewed = wave_field.reshape(forward_dims_of[:3] + (8, len_y))
        forward_section_a = jnp.einsum(
            "pqrmn,pmsk->sqrkn", forward_viewed, w8_fwd, precision=lax.Precision.HIGHEST
        )
        forward_section_b = complex_scale(forward_section_a, twy_fwd[0], twy_fwd[1], 0)
        spectrum_y = jnp.einsum(
            "sqrkn,snth->thkqr", forward_section_b, wy_fwd, precision=lax.Precision.HIGHEST
        )
        spectrum = forward_x(
            lax.all_to_all(spectrum_y, "lat", split_axis=1, concat_axis=4, tiled=True)
        )
        wave_num = frequency[None, :] * references[:, None]
        vertical = (wave_num * wave_num)[:, None, None, :, None, None] - kx_sq - ky_sq
        phase_angle = jnp.sqrt(jnp.maximum(vertical, 0.0)) * depth_step
        damped = jnp.exp(-jnp.sqrt(jnp.maximum(-vertical, 0.0)) * depth_step)
        shifted = complex_scale(
            spectrum[None], damped * jnp.cos(phase_angle), damped * jnp.sin(phase_angle), 1
        )
        inverse_section_c = jnp.einsum(
            "jthkqlo,tosn->jshkqln", shifted, wx_inv, precision=lax.Precision.HIGHEST
        )
        inverse_section_b = complex_scale(inverse_section_c, twx_inv[0], twx_inv[1], 1)
        inverse_section_a = jnp.einsum(
            "jshkqln,slpm->jphkqmn", inverse_section_b, w8_inv, precision=lax.Precision.HIGHEST
        )
        columns = inverse_section_a.reshape(inverse_section_a.shape[:5] + (NX,))
        returned = inverse_y(
            lax.all_to_all(columns, "lat", split_axis=5, concat_axis=2, tiled=True)
        )
        velocity = vel_index[depth_at]
        picked = velocity[None] == jnp.arange(NVEL)[:, None, None]
        local_slow = jnp.sum(jnp.where(picked, table_row[:, None, None], 0.0), 0)
        group_of = velocity // per_group
        split_phase = (
            frequency[None, :, None, None]
            * (local_slow[None, None] - references[:, None, None, None])
            * depth_step
        )
        group_mask = (group_of[None] == jnp.arange(NREF)[:, None, None]).astype(jnp.float32)
        corrected = complex_scale(returned, jnp.cos(split_phase), jnp.sin(split_phase), 1)
        wave_field = jnp.sum(corrected * group_mask[:, None, None], 0)
        summed = jnp.sum(wave_field[0], 0)
        image_rows.append(lax.psum_scatter(summed, "freq", scatter_dimension=1, tiled=True))
    depth_image = jnp.stack(image_rows, 0)
    return (wave_field, depth_image)


def solution(mesh):
    return jax.shard_map(
        local,
        mesh=mesh,
        in_specs=(
            P(None, None, ("freq", "lat")),
            P(("freq", "lat"), None),
            P(("freq", "lat")),
            P(None, ("freq", "lat")),
            P(("freq", "lat")),
            P("freq"),
            P(),
            P(None, "lat", None),
        ),
        out_specs=(P(None, "freq", "lat", None), P(None, "lat", "freq")),
        check_vma=False,
    )
```

profile of v0, /device:TPU:0, one launch (start us, length us, event | category | flops | bytes accessed | tf_op | source)
XLA Modules:
  0.0 646.6 jit_solution(14288893780096186821)
XLA Ops:
  7.2 5.1 sort.17
  16.9 50.7 %while.52 = (s32[]{:T(128)}, u32[1024]{0:T(1024)S(1)}, u32[1024]{0:T(1024)S(1)}, s32[1024]{0:T(1024)S(1)}, s32[]{:T(128)}, /*index=5*/s32[]{:T(128)}, s32[]{}) while((s32[]{:T(128)}, u32[1024]{0:T(1024)S(1)}, u32[1024]{0:T(1024)S(1)}, s32[1024]{0:T(1024)S(1)}, s32[]{:T(128)}, /*index=5*/s32[]{:T(128)}, s32[]{}) %tuple.186), condition=%wide.region_2.3_spmd.clone, body=%wide.region_1.2_spmd.clone.sunk | while | flops 19460 | bytes 67685 | solution.py:107
  76.8 7.3 %all-to-all-start = ((f32[3,1,8,256]{3,1,0,2:T(1,128)}), f32[3,1,8,256]{3,1,0,2:T(1,128)S(1)}, u32[]{:S(2)}, u32[]{:S(2)}) async-start(f32[3,1,8,256]{3,1,0,2:T(1,128)} %copy.348), calls=%async_computation | async-start | bytes 49152 | tf_op jit(solution)/shard_map/all_to_all | solution.py:125
  93.0 26.6 %scatter_fusion = f32[2,4,2048]{1,0,2:T(2,128)S(1)} fusion(f32[2,4,2048]{1,0,2:T(2,128)S(1)} %broadcast.1405, s32[1024]{0:T(1024)S(1)} %broadcast_select_fusion, f32[1024,2,4]{2,1,0:T(2,128)S(1)} %copy.350), kind=kCustom, calls=%fused_computation.4 | custom fusion | bytes 102400
  121.5 6.0 all-to-all-start.1
  129.2 5.2 all-to-all-done.1
  134.4 30.9 %while.51 = (s32[]{:T(128)}, f32[4,8,64,64]{2,3,1,0:T(8,128)}, f32[4,8,64,2,4]{2,1,0,3,4:T(8,128)}, s32[4]{0:T(128)S(1)}, f32[3,1,1,8,256]{4,3,2,1,0:T(8,128)S(1...) while((s32[]{:T(128)}, f32[4,8,64,64]{2,3,1,0:T(8,128)}, ...), condition=%wide.region_7.8_spmd.clone.clone, body=%wide.region_6.7_spmd.clone.clone.sunk | while | flops 28427288 | bytes 1600791 | solution.py:73
  167.1 32.2 %all-reduce.2.cloned.1.call-done = f32[32,64,64]{1,2,0:T(8,128)} async-done(((f32[32,64,64]{1,2,0:T(8,128)}), f32[32,64,64]{1,2,0:T(8,128)}) %all-reduce.2.cloned.1.call-update) | async-done | bytes 524304 | tf_op jit(solution)/shard_map/psum | solution.py:128
  202.1 188.3 %custom-call.11 = f32[32,64,64]{2,1,0:T(8,128)} custom-call(f32[32,64,64]{2,1,0:T(8,128)S(1)} %fusion.24), custom_call_target="Cholesky" | custom-call | tf_op jit(solution)/shard_map/jit(cholesky)/cholesky | solution.py:82
  394.8 67.2 %custom-call.12 = f32[32,1,64,64]{0,2,3,1:T(8,128)S(1)} custom-call(f32[32,1,64,64]{0,3,2,1:T(8,128)} %select_bitcast_fusion), custom_call_target="InvertDiagBlocksLowerTriangular" | custom-call | tf_op jit(solution)/shard_map/jit(_solve_triangular)/vmap()/triangular_solve | solution.py:85
  473.8 5.9 all-to-all-start.2
  480.7 7.5 %all-to-all-done.2 = f32[8,1,8192]{2,1,0:T(1,128)S(1)} async-done(((f32[8,1,8192]{2,1,0:T(1,128)}), f32[8,1,8192]{2,1,0:T(1,128)S(1)}, u32[]{:S(2)}, u32[]{:S(2)}) %all-to-all-start.2) | async-done | bytes 262176 | tf_op jit(solution)/shard_map/all_to_all | solution.py:189
  496.5 4.9 copy.445
  501.4 7.3 %reshape.1555 = f32[8,1,16384]{2,1,0:T(1,128)} reshape(f32[512,1,2,2,8,8]{5,4,3,2,1,0:T(8,128)} %bitcast.594) | data formatting | bytes 1048576
  513.7 12.8 %all-to-all-done.3 = f32[8,1,16384]{2,1,0:T(1,128)S(1)} async-done(((f32[8,1,16384]{2,1,0:T(1,128)}), f32[8,1,16384]{2,1,0:T(1,128)S(1)}, u32[]{:S(2)}, u32[]{:S(2)}) %all-to-all-start.3) | async-done | bytes 524320 | tf_op jit(solution)/shard_map/all_to_all | solution.py:207
  528.4 7.8 %reshape.1556 = f32[512,1,2,2,8,8]{5,4,3,2,1,0:T(8,128)} reshape(f32[8,16384]{1,0:T(8,128)S(1)} %reduce.23) | data formatting | bytes 1048576
  536.2 5.4 copy.379
  548.8 12.5 %all_to_all.70 = f32[8,1,8192]{2,1,0:T(1,128)S(1)} all-to-all(f32[8,1,8192]{2,1,0:T(1,128)S(1)} %reshape.1557), channel_id=1, replica_groups=mesh['freq'=4,'lat'=8] {'lat'}, dimensions={0} | all-to-all | bytes 524288 | tf_op jit(solution)/shard_map/all_to_all | solution.py:189
  569.0 4.9 copy.448
  573.9 7.3 %reshape.1559 = f32[8,1,16384]{2,1,0:T(1,128)} reshape(f32[512,1,2,2,8,8]{5,4,3,2,1,0:T(8,128)} %bitcast.596) | data formatting | bytes 1048576
  585.8 13.1 %all-to-all-done.5 = f32[8,1,16384]{2,1,0:T(1,128)S(1)} async-done(((f32[8,1,16384]{2,1,0:T(1,128)}), f32[8,1,16384]{2,1,0:T(1,128)S(1)}, u32[]{:S(2)}, u32[]{:S(2)}) %all-to-all-start.5) | async-done | bytes 524320 | tf_op jit(solution)/shard_map/all_to_all | solution.py:207
  600.9 7.8 %reshape.1560 = f32[512,1,2,2,8,8]{5,4,3,2,1,0:T(8,128)} reshape(f32[8,16384]{1,0:T(8,128)S(1)} %reduce.25) | data formatting | bytes 1048576
  608.7 5.4 copy.394
  619.4 18.9 %reduce-scatter.8.cloned.1.call-done = f32[64,128]{1,0:T(8,128)} async-done(((f32[64,512]{1,0:T(8,128)}), f32[64,128]{1,0:T(8,128)}) %reduce-scatter.8.cloned.1.call-update) | async-done | bytes 32784 | tf_op jit(solution)/shard_map/reduce_scatter | solution.py:222
  (351 shorter events, 167.4 us)
Async XLA Ops:
  16.8 55.2 %copy-start.41 = (s32[2]{0:T(128)S(1)}, s32[2]{0:T(128)}, u32[]{:S(2)}) copy-start(s32[2]{0:T(128)} %constant.465) | copy-start | bytes 28
  16.9 55.3 %copy-start.40 = (s32[2]{0:T(128)S(1)}, s32[2]{0:T(128)}, u32[]{:S(2)}) copy-start(s32[2]{0:T(128)} %constant.468) | copy-start | bytes 28
  16.9 55.4 %copy-start.28 = (f32[2,1024]{1,0:T(2,128)S(1)}, f32[2,1024]{1,0:T(2,128)}, u32[]{:S(2)}) copy-start(f32[2,1024]{1,0:T(2,128)} %param.39) | copy-start | bytes 24580
  16.9 55.4 %copy-start.29 = (s32[1024]{0:T(1024)S(1)}, s32[1024]{0:T(1024)}, u32[]{:S(2)}) copy-start(s32[1024]{0:T(1024)} %param.38) | copy-start | bytes 12292
  16.9 55.4 %copy-start.30 = (f32[1024]{0:T(1024)S(1)}, f32[1024]{0:T(1024)}, u32[]{:S(2)}) copy-start(f32[1024]{0:T(1024)} %param.40) | copy-start | bytes 12292
  67.6 20.1 %copy-start.39 = (f32[2,8]{1,0:T(2,128)S(1)}, f32[2,8]{1,0:T(2,128)}, u32[]{:S(2)}) copy-start(f32[2,8]{1,0:T(2,128)} %param.42) | copy-start | bytes 196
  67.7 24.2 %copy-start.22 = (f32[2,4,1024]{2,1,0:T(4,128)S(1)}, f32[2,4,1024]{2,1,0:T(4,128)}, u32[]{:S(2)}) copy-start(f32[2,4,1024]{2,1,0:T(4,128)} %param.36) | copy-start | bytes 98308
  76.8 44.7 %all-to-all-start = ((f32[3,1,8,256]{3,1,0,2:T(1,128)}), f32[3,1,8,256]{3,1,0,2:T(1,128)S(1)}, u32[]{:S(2)}, u32[]{:S(2)}) async-start(f32[3,1,8,256]{3,1,0,2:T(1,128)} %copy.348), calls=%async_computation | async-start | bytes 49152 | tf_op jit(solution)/shard_map/all_to_all | solution.py:125
  121.5 12.9 %all-to-all-start.1 = ((f32[2,4,8,256]{3,1,0,2:T(4,128)}), f32[2,4,8,256]{3,1,0,2:T(4,128)S(1)}, u32[]{:S(2)}, u32[]{:S(2)}) async-start(f32[2,4,8,256]{3,1,0,2:T(4,128)} %copy.351), calls=%async_computation.1 | async-start | bytes 131072 | tf_op jit(solution)/shard_map/all_to_all | solution.py:124
  127.5 71.8 %all-reduce.2.cloned.1.call-start = ((), (), s32[]{:S(2)}) async-start(), calls=%async_computation.9 | async-start | bytes 2097152 | tf_op jit(solution)/shard_map/psum | solution.py:128
  134.4 31.2 %copy-start.13 = (f32[64,64]{1,0:T(8,128)S(1)}, f32[64,64]{1,0:T(8,128)}, u32[]{:S(2)}) copy-start(f32[64,64]{1,0:T(8,128)} %fusion.111) | copy-start | bytes 49156
  134.4 31.3 %copy-start.26 = (f32[1,8,2,8]{3,1,2,0:T(8,128)S(1)}, f32[1,8,2,8]{3,1,2,0:T(8,128)}, u32[]{:S(2)}) copy-start(f32[1,8,2,8]{3,1,2,0:T(8,128)} %get-tuple-element.409) | copy-start | bytes 1540
  134.4 31.4 %copy-start.25 = (f32[1,8,2,8]{3,1,2,0:T(8,128)S(1)}, f32[1,8,2,8]{3,1,2,0:T(8,128)}, u32[]{:S(2)}) copy-start(f32[1,8,2,8]{3,1,2,0:T(8,128)} %get-tuple-element.408) | copy-start | bytes 1540
  165.4 298.2 %reduce-scatter.4.cloned.1.call-start = ((), (), s32[]{:S(2)}) async-start(), calls=%async_computation.10 | async-start | bytes 163840 | tf_op jit(solution)/shard_map/reduce_scatter | solution.py:129
  165.7 33.6 %copy-start.5 = (f32[64,64]{0,1:T(8,128)}, f32[64,64]{0,1:T(8,128)S(1)}, u32[]{:S(2)}) copy-start(f32[64,64]{0,1:T(8,128)S(1)} %copy.355) | copy-start | bytes 49156
  473.8 14.4 %all-to-all-start.2 = ((f32[8,1,8192]{2,1,0:T(1,128)}), f32[8,1,8192]{2,1,0:T(1,128)S(1)}, u32[]{:S(2)}, u32[]{:S(2)}) async-start(f32[8,1,8192]{2,1,0:T(1,128)} %reshape.1553), calls=%async_computation.3 | async-start | bytes 524288 | tf_op jit(solution)/shard_map/all_to_all | solution.py:189
  479.9 15.6 %copy-start.9 = (f32[1,8,2,8]{1,3,0,2:T(8,128)}, f32[1,8,2,8]{1,3,0,2:T(8,128)S(1)}, u32[]{:S(2)}) copy-start(f32[1,8,2,8]{1,3,0,2:T(8,128)S(1)} %copy.342) | copy-start | bytes 1540
  479.9 15.5 %copy-start.11 = (f32[1,8,2,8]{1,3,0,2:T(8,128)}, f32[1,8,2,8]{1,3,0,2:T(8,128)S(1)}, u32[]{:S(2)}) copy-start(f32[1,8,2,8]{1,3,0,2:T(8,128)S(1)} %copy.343) | copy-start | bytes 1540
  480.0 11.9 %copy-start.17 = (f32[8,8]{1,0:T(8,128)}, f32[8,8]{1,0:T(8,128)S(1)}, u32[]{:S(2)}) copy-start(f32[8,8]{1,0:T(8,128)S(1)} %fusion.131) | copy-start | bytes 772
  508.8 17.7 %all-to-all-start.3 = ((f32[8,1,16384]{2,1,0:T(1,128)}), f32[8,1,16384]{2,1,0:T(1,128)S(1)}, u32[]{:S(2)}, u32[]{:S(2)}) async-start(f32[8,1,16384]{2,1,0:T(1,128)} %reshape.1555), calls=%async_computation.4 | async-start | bytes 1048576 | tf_op jit(solution)/shard_map/all_to_all | solution.py:207
  581.2 17.8 %all-to-all-start.5 = ((f32[8,1,16384]{2,1,0:T(1,128)}), f32[8,1,16384]{2,1,0:T(1,128)S(1)}, u32[]{:S(2)}, u32[]{:S(2)}) async-start(f32[8,1,16384]{2,1,0:T(1,128)} %reshape.1559), calls=%async_computation.6 | async-start | bytes 1048576 | tf_op jit(solution)/shard_map/all_to_all | solution.py:207
  584.8 34.6 %reduce-scatter.6.cloned.1.call-start = ((), (), s32[]{:S(2)}) async-start(), calls=%async_computation.11 | async-start | bytes 163840 | tf_op jit(solution)/shard_map/reduce_scatter | solution.py:222
  585.5 52.7 %reduce-scatter.8.cloned.1.call-start = ((), (), s32[]{:S(2)}) async-start(), calls=%async_computation.12 | async-start | bytes 163840 | tf_op jit(solution)/shard_map/reduce_scatter | solution.py:222
  618.6 21.0 %copy-start.2 = (f32[2,64,512]{2,1,0:T(8,128)}, f32[2,64,512]{2,1,0:T(8,128)S(1)}, u32[]{:S(2)}) copy-start(f32[2,64,512]{2,1,0:T(8,128)S(1)} %fusion.46) | copy-start | bytes 786436
  (27 other events, 117.4 us)
Sparse Core Ops, SparseCore 0:
  165.5 33.8 all-reduce.1
  202.3 20.4 reduce-scatter.3
  588.0 21.0 reduce-scatter.5
  619.5 18.7 reduce-scatter.7
where the time goes:
time: 656 us; the launch traced here: 647 us
  other arithmetic  302 us (46%)
  local copies, waits for them, and re-layouts  166 us (25%)
  waiting for transfers between devices  89.8 us (14%)
  matrix products  29.4 us (4%)
  starting transfers between devices  27.1 us (4%)
  between operations  16.1 us (2%)
  blocking collectives  12.5 us (2%)
    another operation x4, other arithmetic, fit_grid(): factor = jnp.linalg.cholesky(system)  190 us
    another operation x3, other arithmetic, fit_grid(): jax.scipy.linalg.solve_triangular(factor, middle, lower=True, trans='T')  69.5 us
    unnamed x96, local copies, waits for them, and re-layouts  63.4 us
    gather x11, local copies, waits for them, and re-layouts, local(): firsts = jnp.searchsorted(sorted_tiles, sorted_tiles, side='left')  49.8 us
    psum x1, waiting for transfers between devices, local(): normal = lax.psum(normal, 'freq')  32.2 us
    all_to_all x2, waiting for transfers between devices, local(): lax.all_to_all(columns, 'lat', split_axis=5, concat_axis=2, tiled=True)  25.9 us
    reduce_scatter x2, waiting for transfers between devices, local(): lax.psum_scatter(summed, 'freq', scatter_dimension=1, tiled=True)  18.9 us
  transfers between devices with their start and end apart: 9, of which 6 were waited for; matrix products, arithmetic and copies ran while one was open for 51% of the time, Pallas kernels for 0%

commit v1 on v0

--- a/solution.py
+++ b/solution.py
@@ -204,7 +204,12 @@
         )
         columns = inverse_section_a.reshape(inverse_section_a.shape[:5] + (NX,))
         returned = inverse_y(
-            lax.all_to_all(columns, "lat", split_axis=5, concat_axis=2, tiled=True)
+            jnp.concatenate(
+                lax.all_to_all(
+                    jnp.stack(jnp.split(columns, lax.axis_size("lat"), axis=5)), "lat", 0, 0
+                ),
+                axis=2,
+            )
         )
         velocity = vel_index[depth_at]
         picked = velocity[None] == jnp.arange(NVEL)[:, None, None]

time: 656 us -> 616 us (0.939)
  local copies, waits for them, and re-layouts: 166 us -> 121 us
    unnamed x96 -> x116, local copies, waits for them, and re-layouts: 63.4 us -> 37.5 us
    all_to_all x2 -> x0, local copies, waits for them, and re-layouts: 10.8 us -> none  [local(): lax.all_to_all(columns, 'lat', split_axis=5, concat_axis=2, tiled=True)]
    reshape x2, local copies, waits for them, and re-layouts: 9.87 us -> 0.54 us  [local(): columns = inverse_section_a.reshape(inverse_section_a.shape[:5] + (NX,))]
  transfers between devices with their start and end apart: 9 -> 9, of which waited for: 6 -> 7; matrix products, arithmetic and copies ran while one was open for 51% -> 52% of each run, Pallas kernels for 0% -> 0%
where the time goes in v1:
time: 616 us; the launch traced here: 607 us
  other arithmetic  303 us (49%)
  local copies, waits for them, and re-layouts  121 us (20%)
  waiting for transfers between devices  94.5 us (15%)
  matrix products  30.4 us (5%)
  starting transfers between devices  27.1 us (4%)
  between operations  16.1 us (3%)
  blocking collectives  12.4 us (2%)
    another operation x4, other arithmetic, fit_grid(): factor = jnp.linalg.cholesky(system)  190 us
    another operation x3, other arithmetic, fit_grid(): jax.scipy.linalg.solve_triangular(factor, middle, lower=True, trans='T')  69.6 us
    gather x11, local copies, waits for them, and re-layouts, local(): firsts = jnp.searchsorted(sorted_tiles, sorted_tiles, side='left')  49.8 us
    unnamed x116, local copies, waits for them, and re-layouts  37.5 us
    psum x1, waiting for transfers between devices, local(): normal = lax.psum(normal, 'freq')  32.3 us
    all_to_all x2, waiting for transfers between devices, local(): lax.all_to_all(jnp.stack(jnp.split(columns, lax.axis_size('lat'), axis=5)...  25.1 us
    reduce_scatter x2, waiting for transfers between devices, local(): lax.psum_scatter(summed, 'freq', scatter_dimension=1, tiled=True)  24.3 us
    all_to_all x1, blocking collectives, local(): lax.all_to_all(spectrum_y, 'lat', split_axis=1, concat_axis=4, tiled=True)  12.4 us
  transfers between devices with their start and end apart: 9, of which 7 were waited for; matrix products, arithmetic and copies ran while one was open for 52% of the time, Pallas kernels for 0%

profile of v1, /device:TPU:0, one launch (start us, length us, event | category | flops | bytes accessed | tf_op | source)
XLA Modules:
  0.0 607.4 jit_solution(3074003097794449078)
XLA Ops:
  7.2 5.1 sort.17
  12.3 4.5 gather_fusion.1
  16.9 50.7 %while.52 = (s32[]{:T(128)}, u32[1024]{0:T(1024)S(1)}, u32[1024]{0:T(1024)S(1)}, s32[1024]{0:T(1024)S(1)}, s32[]{:T(128)}, /*index=5*/s32[]{:T(128)}, s32[]{}) while((s32[]{:T(128)}, u32[1024]{0:T(1024)S(1)}, u32[1024]{0:T(1024)S(1)}, s32[1024]{0:T(1024)S(1)}, s32[]{:T(128)}, /*index=5*/s32[]{:T(128)}, s32[]{}) %tuple.186), condition=%wide.region_2.3_spmd.clone, body=%wide.region_1.2_spmd.clone.sunk | while | flops 19460 | bytes 67685 | solution.py:107
  16.9 4.5 gather_fusion
  21.5 4.5 gather_fusion
  26.2 4.5 gather_fusion
  30.8 4.5 gather_fusion
  35.4 4.5 gather_fusion
  40.0 4.5 gather_fusion
  49.2 4.5 gather_fusion
  76.8 7.3 %all-to-all-start = ((f32[3,1,8,256]{3,1,0,2:T(1,128)}), f32[3,1,8,256]{3,1,0,2:T(1,128)S(1)}, u32[]{:S(2)}, u32[]{:S(2)}) async-start(f32[3,1,8,256]{3,1,0,2:T(1,128)} %copy.340), calls=%async_computation | async-start | bytes 49152 | tf_op jit(solution)/shard_map/all_to_all | solution.py:125
  93.0 26.6 %scatter_fusion = f32[2,4,2048]{1,0,2:T(2,128)S(1)} fusion(f32[2,4,2048]{1,0,2:T(2,128)S(1)} %broadcast.1405, s32[1024]{0:T(1024)S(1)} %broadcast_select_fusion, f32[1024,2,4]{2,1,0:T(2,128)S(1)} %copy.342), kind=kCustom, calls=%fused_computation.4 | custom fusion | bytes 102400
  121.5 6.0 all-to-all-start.1
  129.2 5.2 all-to-all-done.1
  134.4 31.0 %while.51 = (s32[]{:T(128)}, f32[4,8,64,64]{2,3,1,0:T(8,128)}, f32[4,8,64,2,4]{2,1,0,3,4:T(8,128)}, s32[4]{0:T(128)S(1)}, f32[3,1,1,8,256]{4,3,2,1,0:T(8,128)S(1...) while((s32[]{:T(128)}, f32[4,8,64,64]{2,3,1,0:T(8,128)}, ...), condition=%wide.region_7.8_spmd.clone.clone, body=%wide.region_6.7_spmd.clone.clone.sunk | while | flops 28427288 | bytes 1600791 | solution.py:73
  167.1 32.3 %all-reduce.2.cloned.1.call-done = f32[32,64,64]{1,2,0:T(8,128)} async-done(((f32[32,64,64]{1,2,0:T(8,128)}), f32[32,64,64]{1,2,0:T(8,128)}) %all-reduce.2.cloned.1.call-update) | async-done | bytes 524304 | tf_op jit(solution)/shard_map/psum | solution.py:128
  202.2 188.3 %custom-call.11 = f32[32,64,64]{2,1,0:T(8,128)} custom-call(f32[32,64,64]{2,1,0:T(8,128)S(1)} %fusion.24), custom_call_target="Cholesky" | custom-call | tf_op jit(solution)/shard_map/jit(cholesky)/cholesky | solution.py:82
  394.9 67.2 %custom-call.12 = f32[32,1,64,64]{0,2,3,1:T(8,128)S(1)} custom-call(f32[32,1,64,64]{0,3,2,1:T(8,128)} %select_bitcast_fusion), custom_call_target="InvertDiagBlocksLowerTriangular" | custom-call | tf_op jit(solution)/shard_map/jit(_solve_triangular)/vmap()/triangular_solve | solution.py:85
  474.0 5.8 all-to-all-start.2
  480.6 7.5 %all-to-all-done.2 = f32[8,1,8192]{2,1,0:T(1,128)S(1)} async-done(((f32[8,1,8192]{2,1,0:T(1,128)}), f32[8,1,8192]{2,1,0:T(1,128)S(1)}, u32[]{:S(2)}, u32[]{:S(2)}) %all-to-all-start.2) | async-done | bytes 262176 | tf_op jit(solution)/shard_map/all_to_all | solution.py:189
  504.7 12.0 %all-to-all-done.3 = f32[8,1,16384]{2,1,0:T(1,128)S(1)} async-done(((f32[8,1,16384]{2,1,0:T(1,128)}), f32[8,1,16384]{2,1,0:T(1,128)S(1)}, u32[]{:S(2)}, u32[]{:S(2)}) %all-to-all-start.3) | async-done | bytes 524320 | tf_op jit(solution)/shard_map/all_to_all | solution.py:208
  527.0 12.4 %all_to_all.50 = f32[8,1,8192]{2,1,0:T(1,128)S(1)} all-to-all(f32[8,1,8192]{2,1,0:T(1,128)S(1)} %reshape.1567), channel_id=1, replica_groups=mesh['freq'=4,'lat'=8] {'lat'}, dimensions={0} | all-to-all | bytes 524288 | tf_op jit(solution)/shard_map/all_to_all | solution.py:189
  554.0 13.2 %all-to-all-done.5 = f32[8,1,16384]{2,1,0:T(1,128)S(1)} async-done(((f32[8,1,16384]{2,1,0:T(1,128)}), f32[8,1,16384]{2,1,0:T(1,128)S(1)}, u32[]{:S(2)}, u32[]{:S(2)}) %all-to-all-start.5) | async-done | bytes 524320 | tf_op jit(solution)/shard_map/all_to_all | solution.py:208
  577.3 21.9 %reduce-scatter.8.cloned.1.call-done = f32[64,128]{1,0:T(8,128)} async-done(((f32[64,512]{1,0:T(8,128)}), f32[64,128]{1,0:T(8,128)}) %reduce-scatter.8.cloned.1.call-update) | async-done | bytes 32784 | tf_op jit(solution)/shard_map/reduce_scatter | solution.py:227
  (373 shorter events, 140.8 us)
Async XLA Ops:
  16.8 55.2 %copy-start.44 = (s32[2]{0:T(128)S(1)}, s32[2]{0:T(128)}, u32[]{:S(2)}) copy-start(s32[2]{0:T(128)} %constant.465) | copy-start | bytes 28
  16.9 55.3 %copy-start.43 = (s32[2]{0:T(128)S(1)}, s32[2]{0:T(128)}, u32[]{:S(2)}) copy-start(s32[2]{0:T(128)} %constant.468) | copy-start | bytes 28
  16.9 55.4 %copy-start.31 = (f32[2,1024]{1,0:T(2,128)S(1)}, f32[2,1024]{1,0:T(2,128)}, u32[]{:S(2)}) copy-start(f32[2,1024]{1,0:T(2,128)} %param.39) | copy-start | bytes 24580
  16.9 55.4 %copy-start.32 = (s32[1024]{0:T(1024)S(1)}, s32[1024]{0:T(1024)}, u32[]{:S(2)}) copy-start(s32[1024]{0:T(1024)} %param.38) | copy-start | bytes 12292
  16.9 55.4 %copy-start.33 = (f32[1024]{0:T(1024)S(1)}, f32[1024]{0:T(1024)}, u32[]{:S(2)}) copy-start(f32[1024]{0:T(1024)} %param.40) | copy-start | bytes 12292
  67.6 20.2 %copy-start.42 = (f32[2,8]{1,0:T(2,128)S(1)}, f32[2,8]{1,0:T(2,128)}, u32[]{:S(2)}) copy-start(f32[2,8]{1,0:T(2,128)} %param.42) | copy-start | bytes 196
  67.7 24.2 %copy-start.25 = (f32[2,4,1024]{2,1,0:T(4,128)S(1)}, f32[2,4,1024]{2,1,0:T(4,128)}, u32[]{:S(2)}) copy-start(f32[2,4,1024]{2,1,0:T(4,128)} %param.36) | copy-start | bytes 98308
  76.8 44.6 %all-to-all-start = ((f32[3,1,8,256]{3,1,0,2:T(1,128)}), f32[3,1,8,256]{3,1,0,2:T(1,128)S(1)}, u32[]{:S(2)}, u32[]{:S(2)}) async-start(f32[3,1,8,256]{3,1,0,2:T(1,128)} %copy.340), calls=%async_computation | async-start | bytes 49152 | tf_op jit(solution)/shard_map/all_to_all | solution.py:125
  121.5 12.9 %all-to-all-start.1 = ((f32[2,4,8,256]{3,1,0,2:T(4,128)}), f32[2,4,8,256]{3,1,0,2:T(4,128)S(1)}, u32[]{:S(2)}, u32[]{:S(2)}) async-start(f32[2,4,8,256]{3,1,0,2:T(4,128)} %copy.343), calls=%async_computation.1 | async-start | bytes 131072 | tf_op jit(solution)/shard_map/all_to_all | solution.py:124
  127.5 72.0 %all-reduce.2.cloned.1.call-start = ((), (), s32[]{:S(2)}) async-start(), calls=%async_computation.9 | async-start | bytes 2097152 | tf_op jit(solution)/shard_map/psum | solution.py:128
  134.4 31.3 %copy-start.16 = (f32[64,64]{1,0:T(8,128)S(1)}, f32[64,64]{1,0:T(8,128)}, u32[]{:S(2)}) copy-start(f32[64,64]{1,0:T(8,128)} %fusion.129) | copy-start | bytes 49156
  134.4 31.3 %copy-start.29 = (f32[1,8,2,8]{3,1,2,0:T(8,128)S(1)}, f32[1,8,2,8]{3,1,2,0:T(8,128)}, u32[]{:S(2)}) copy-start(f32[1,8,2,8]{3,1,2,0:T(8,128)} %get-tuple-element.409) | copy-start | bytes 1540
  134.4 31.4 %copy-start.28 = (f32[1,8,2,8]{3,1,2,0:T(8,128)S(1)}, f32[1,8,2,8]{3,1,2,0:T(8,128)}, u32[]{:S(2)}) copy-start(f32[1,8,2,8]{3,1,2,0:T(8,128)} %get-tuple-element.408) | copy-start | bytes 1540
  165.4 298.3 %reduce-scatter.4.cloned.1.call-start = ((), (), s32[]{:S(2)}) async-start(), calls=%async_computation.10 | async-start | bytes 163840 | tf_op jit(solution)/shard_map/reduce_scatter | solution.py:129
  165.7 33.7 %copy-start.7 = (f32[64,64]{0,1:T(8,128)}, f32[64,64]{0,1:T(8,128)S(1)}, u32[]{:S(2)}) copy-start(f32[64,64]{0,1:T(8,128)S(1)} %copy.347) | copy-start | bytes 49156
  165.8 305.0 %copy-start.11 = (f32[1,8,2,8]{1,3,0,2:T(8,128)}, f32[1,8,2,8]{1,3,0,2:T(8,128)S(1)}, u32[]{:S(2)}) copy-start(f32[1,8,2,8]{1,3,0,2:T(8,128)S(1)} %copy.337) | copy-start | bytes 1540
  472.6 17.6 %copy-start.12 = (f32[1,8,2,8]{1,3,0,2:T(8,128)S(1)}, f32[1,8,2,8]{1,3,0,2:T(8,128)}, u32[]{:S(2)}) copy-start(f32[1,8,2,8]{1,3,0,2:T(8,128)} %copy-done.11) | copy-start | bytes 1540
  474.0 14.2 %all-to-all-start.2 = ((f32[8,1,8192]{2,1,0:T(1,128)}), f32[8,1,8192]{2,1,0:T(1,128)S(1)}, u32[]{:S(2)}, u32[]{:S(2)}) async-start(f32[8,1,8192]{2,1,0:T(1,128)} %reshape.1563), calls=%async_computation.3 | async-start | bytes 524288 | tf_op jit(solution)/shard_map/all_to_all | solution.py:189
  479.9 15.5 %copy-start.9 = (f32[1,8,2,8]{1,3,0,2:T(8,128)}, f32[1,8,2,8]{1,3,0,2:T(8,128)S(1)}, u32[]{:S(2)}) copy-start(f32[1,8,2,8]{1,3,0,2:T(8,128)S(1)} %copy.335) | copy-start | bytes 1540
  498.7 17.9 %all-to-all-start.3 = ((f32[8,1,16384]{2,1,0:T(1,128)}), f32[8,1,16384]{2,1,0:T(1,128)S(1)}, u32[]{:S(2)}, u32[]{:S(2)}) async-start(f32[8,1,16384]{2,1,0:T(1,128)} %reshape.1565), calls=%async_computation.4 | async-start | bytes 1048576 | tf_op jit(solution)/shard_map/all_to_all | solution.py:208
  549.4 17.8 %all-to-all-start.5 = ((f32[8,1,16384]{2,1,0:T(1,128)}), f32[8,1,16384]{2,1,0:T(1,128)S(1)}, u32[]{:S(2)}, u32[]{:S(2)}) async-start(f32[8,1,16384]{2,1,0:T(1,128)} %reshape.1569), calls=%async_computation.6 | async-start | bytes 1048576 | tf_op jit(solution)/shard_map/all_to_all | solution.py:208
  553.0 24.3 %reduce-scatter.6.cloned.1.call-start = ((), (), s32[]{:S(2)}) async-start(), calls=%async_computation.11 | async-start | bytes 163840 | tf_op jit(solution)/shard_map/reduce_scatter | solution.py:227
  553.7 45.5 %reduce-scatter.8.cloned.1.call-start = ((), (), s32[]{:S(2)}) async-start(), calls=%async_computation.12 | async-start | bytes 163840 | tf_op jit(solution)/shard_map/reduce_scatter | solution.py:227
  574.2 26.5 %copy-start.4 = (f32[2,64,512]{2,1,0:T(8,128)}, f32[2,64,512]{2,1,0:T(8,128)S(1)}, u32[]{:S(2)}) copy-start(f32[2,64,512]{2,1,0:T(8,128)S(1)} %fusion.48) | copy-start | bytes 786436
  (30 other events, 121.3 us)
Sparse Core Ops, SparseCore 0:
  165.5 33.8 all-reduce.1
  202.4 20.4 reduce-scatter.3
  556.2 21.0 reduce-scatter.5
  579.6 19.6 reduce-scatter.7
